TPU v7x, 256 devices: a 4x2x16 block of a 4x16x16 slice. The times are simulated.
256 devices in a mesh: parts: 2 (over y), rows: 128 (over z, x, core).
Axes of the slice: x: 4, y: 2, z: 16, core: 2. Of those that a mesh axis runs over, the one named last changes fastest.
The devices are a block of a 4x16x16 slice.
Arguments:
- latent: bfloat16 [4, 128, 160, 384], P('parts', 'rows'), parts along dimension 0, may hold values from -40 to 40
- conv_cache: bfloat16 [4, 128, 160, 384], P('parts', 'rows'), parts along dimension 0, may hold values from -6 to 6
- time_cache: bfloat16 [4, 128, 160, 384], P('parts', 'rows'), parts along dimension 0, may hold values from -6 to 6
- norm_gain: float32 [384], replicated, may hold values from 0.5 to 2
- norm_shift: float32 [384], replicated, may hold values from -3 to 3
- conv_weight: bfloat16 [3, 3, 3, 384, 384], replicated, may hold values from -0.0625 to 0.0625
- conv_bias: float32 [384], replicated, may hold values from -2 to 2
- time_weight: bfloat16 [3, 384, 768], replicated, may hold values from -0.1875 to 0.1875
- time_bias: float32 [768], replicated, may hold values from -2 to 2
- up_weight: bfloat16 [3, 3, 384, 192], replicated, may hold values from -0.109375 to 0.109375
- up_bias: float32 [192], replicated, may hold values from -2 to 2
Outputs:
- frames_out: bfloat16 [8, 256, 320, 192], P('parts', 'rows'), parts along dimension 0
There are 2 independent parts, one for each index of `parts`. A program takes and returns all parts, laid end to end along the dimension named above; an argument that names none is the same for every part. Nothing has to cross between parts.
All inputs are finite; a program needn't handle non-finite values.
Results may differ from a plain program's by a relative error of at most 0.0056.
Values may be sent and summed in bfloat16 or wider, within the bound.
No kernel may reach another device: no remote copies, remote signals or barrier semaphores. Data moves between devices by JAX's collectives and lax.ppermute only.
A program may use at most 64 MiB of HBM per device.

v0:
```python
import jax
import jax.numpy as jnp
from jax import lax
from jax.sharding import Mesh
from jax.sharding import PartitionSpec as P

GROUPS = 32
ROWS = ("rows_0", "rows_1", "rows_2")
EPSILON = 1e-06


def over_axes(value, axes):
    for axis in axes:
        value = lax.psum(value, axis)
    return value


def with_halo(value, sides, width):
    for axis, dim in sides:
        devices, length = (lax.axis_size(axis), value.shape[dim])
        up = [(i, (i + 1) % devices) for i in range(devices - 1)]
        down = [(j, i) for i, j in up]
        last = lax.slice_in_dim(value, length - width, length, axis=dim)
        initial = lax.slice_in_dim(value, 0, width, axis=dim)
        before = lax.ppermute(last, axis, up)
        after = lax.ppermute(initial, axis, down)
        value = jnp.concatenate([before, value, after], axis=dim)
    return value


def conv_taps(padded, kernel, row_count, col_count):
    channels = padded.shape[-1]
    total = jnp.zeros((padded.shape[0] * row_count * col_count, kernel.shape[-1]), jnp.float32)
    for row_tap in range(3):
        window = jnp.concatenate(
            [
                padded[:, row_tap : row_tap + row_count, col_tap : col_tap + col_count]
                for col_tap in range(3)
            ],
            axis=-1,
        )
        total = total + jnp.dot(
            window.reshape(-1, 3 * channels),
            kernel[row_tap].reshape(3 * channels, -1),
            preferred_element_type=jnp.float32,
        )
    return total


def temporal(block, time_cache, time_weight, time_bias):
    frame_count = block.shape[0]
    channels = block.shape[-1]
    joined = jnp.concatenate([time_cache, block], axis=0)
    window = jnp.concatenate(
        [joined[frame_tap : frame_tap + frame_count] for frame_tap in range(3)], axis=-1
    )
    mixed = (
        jnp.dot(
            window.reshape(-1, 3 * channels),
            time_weight.reshape(3 * channels, -1),
            preferred_element_type=jnp.float32,
        )
        + time_bias
    )
    mixed = mixed.astype(jnp.bfloat16).reshape(block.shape[:-1] + (2, channels))
    return jnp.moveaxis(mixed, 3, 1).reshape((2 * frame_count,) + block.shape[1:])


def on_device(
    latent,
    conv_cache,
    time_cache,
    norm_gain,
    norm_shift,
    conv_weight,
    conv_bias,
    time_weight,
    time_bias,
    up_weight,
    up_bias,
):
    frame_count, row_count, col_count, channels = latent.shape
    signal = latent.astype(jnp.float32)
    grouped = signal.reshape(frame_count, row_count, col_count, GROUPS, channels // GROUPS)
    entries = float(
        frame_count * row_count * lax.axis_size(ROWS) * col_count * (channels // GROUPS)
    )
    total_sum, square_sum = (
        over_axes(jnp.sum(grouped, axis=(0, 1, 2, 4)), ROWS),
        over_axes(jnp.sum(grouped * grouped, axis=(0, 1, 2, 4)), ROWS),
    )
    center = (total_sum / entries).reshape(1, 1, 1, GROUPS, 1)
    spread = square_sum.reshape(1, 1, 1, GROUPS, 1) / entries - center * center
    normed = ((grouped - center) * lax.rsqrt(spread + EPSILON)).reshape(signal.shape)
    active = jax.nn.silu(normed * norm_gain + norm_shift).astype(jnp.bfloat16)
    joined = jnp.concatenate([conv_cache, active], axis=0)
    rimmed = with_halo(joined, ((ROWS, 1),), 1)
    padded = jnp.pad(rimmed, ((0, 0), (0, 0), (1, 1), (0, 0)))
    summed = conv_bias + jnp.zeros((frame_count * row_count * col_count, channels), jnp.float32)
    for frame_tap in range(3):
        summed = summed + conv_taps(
            padded[frame_tap : frame_tap + frame_count],
            conv_weight[frame_tap],
            row_count,
            col_count,
        )
    block = (signal + summed.reshape(signal.shape)).astype(jnp.bfloat16)
    doubled = temporal(block, time_cache, time_weight, time_bias)
    upsampled = jnp.repeat(jnp.repeat(doubled, 2, axis=1), 2, axis=2)
    upsampled = with_halo(upsampled, ((ROWS, 1),), 1)
    padded_up = jnp.pad(upsampled, ((0, 0), (0, 0), (1, 1), (0, 0)))
    result = conv_taps(padded_up, up_weight, 2 * row_count, 2 * col_count) + up_bias
    return result.astype(jnp.bfloat16).reshape(
        2 * frame_count, 2 * row_count, 2 * col_count, up_weight.shape[-1]
    )


def solution(mesh):
    finer = Mesh(
        mesh.devices.reshape(mesh.shape["parts"], 16, 4, 2), ("parts", "rows_0", "rows_1", "rows_2")
    )
    placed = (
        P("parts", ROWS, None, None),
        P("parts", ROWS, None, None),
        P("parts", ROWS, None, None),
        P(),
        P(),
        P(),
        P(),
        P(),
        P(),
        P(),
        P(),
    )
    return jax.shard_map(
        on_device,
        mesh=finer,
        in_specs=placed,
        out_specs=P("parts", ROWS, None, None),
        check_vma=False,
    )
```

profile of v0, /device:TPU:39, one launch (start us, length us, event | category | flops | bytes accessed | tf_op | source)
XLA Modules:
  0.0 134.7 jit_solution(4475981144398984496)
XLA Ops:
  0.0 1.2 convert_reduce_fusion
  1.2 0.1 reduce_sum.24
  1.3 0.1 reduce_sum.36
  1.4 0.1 reduce_sum.25
  1.5 0.1 reduce_sum.37
  1.6 42.4 %all-reduce.2 = (f32[32]{0:T(128)S(1)}, f32[32]{0:T(128)S(1)}) all-reduce(f32[32]{0:T(128)S(1)} %reduce_sum.37, f32[32]{0:T(128)S(1)} %reduce_sum.25), channel_id=1, replica_groups=mesh['parts'=2,'rows_0'=16,'rows_1'=4,'rows_2'=2] {'rows_0'}, use_global_device_ids=true, to_apply=%region_7.0 | all-reduce | flops 64 | bytes 512 | tf_op jit(solution)/shard_map/psum | solution.py:14
  44.0 5.8 %all-reduce.3 = (f32[32]{0:T(128)S(1)}, f32[32]{0:T(128)S(1)}) all-reduce(f32[32]{0:T(128)S(1)} %get-tuple-element.7, f32[32]{0:T(128)S(1)} %get-tuple-element.8), channel_id=1, replica_groups=mesh['parts'=2,'rows_0'=16,'rows_1'=4,'rows_2'=2] {'rows_1'}, use_global_device_ids=true, to_apply=%region_8.9 | all-reduce | flops 64 | bytes 512 | tf_op jit(solution)/shard_map/psum | solution.py:14
  49.8 11.5 %all-reduce.4 = (f32[32]{0:T(128)S(1)}, f32[32]{0:T(128)S(1)}) all-reduce(f32[32]{0:T(128)S(1)} %get-tuple-element.9, f32[32]{0:T(128)S(1)} %get-tuple-element.10), channel_id=1, replica_groups=mesh['parts'=2,'rows_0'=16,'rows_1'=4,'rows_2'=2] {'rows_2'}, use_global_device_ids=true, to_apply=%region_9.10 | all-reduce | flops 64 | bytes 512 | tf_op jit(solution)/shard_map/psum | solution.py:14
  61.3 0.1 mul.44
  61.4 0.1 mul.45
  61.5 0.1 sub.20
  61.6 0.1 sub.21
  61.7 1.1 fusion.31
  62.9 1.0 pad_maximum_fusion.13
  63.9 3.8 %collective-permute-start = (bf16[4,1,160,384]{3,2,1,0:T(8,128)(2,1)S(1)}, bf16[4,1,160,384]{3,2,1,0:T(8,128)(2,1)S(1)}, u32[]{:S(2)}, u32[]{:S(2)}) collective-permute-start(bf16[4,1,160,384]{3,2,1,0:T(8,128)(2,1)S(1)} %pad_maximum_fusion.13), channel_id=1, source_target_pairs={{0,1},{1,2},{2,3},{3,4},{4,5},{5,6},{6,7},{7,8},{8,9},{9,10},{10,1... | collective-permute-start | bytes 1474568 | tf_op jit(solution)/shard_map/ppermute | solution.py:25
  67.6 2.0 %collective-permute-start.1 = (bf16[4,1,160,384]{3,2,1,0:T(8,128)(2,1)S(1)}, bf16[4,1,160,384]{3,2,1,0:T(8,128)(2,1)S(1)}, u32[]{:S(2)}, u32[]{:S(2)}) collective-permute-start(bf16[4,1,160,384]{3,2,1,0:T(8,128)(2,1)S(1)} %pad_maximum_fusion.13), channel_id=1, source_target_pairs={{1,0},{2,1},{3,2},{4,3},{5,4},{6,5},{7,6},{8,7},{9,8},{10,9},{11,1... | collective-permute-start | bytes 1474568 | tf_op jit(solution)/shard_map/ppermute | solution.py:26
  69.6 3.9 %fusion.35 = (bf16[1,1,3,384,384]{4,3,2,1,0:T(8,128)(2,1)S(1)}, bf16[1,1,3,384,384]{4,3,2,1,0:T(8,128)(2,1)S(1)}, bf16[1,1,3,384,384]{4,3,2,1,0:T(8,128)(2,1)S(1...) fusion(bf16[3,3,3,384,384]{4,3,2,1,0:T(8,128)(2,1)} %param.16), kind=kLoop, calls=%fused_computation.71 | loop fusion | bytes 15925248 | tf_op jit(solution)/shard_map/slice | solution.py:44
  73.6 6.3 %collective-permute-done.1 = bf16[4,1,160,384]{3,2,1,0:T(8,128)(2,1)S(1)} collective-permute-done((bf16[4,1,160,384]{3,2,1,0:T(8,128)(2,1)S(1)}, bf16[4,1,160,384]{3,2,1,0:T(8,128)(2,1)S(1)}, u32[]{:S(2)}, u32[]{:S(2)}) %collective-permute-start.1) | collective-permute-done | bytes 491552 | tf_op jit(solution)/shard_map/ppermute | solution.py:26
  79.9 0.5 select_maximum_fusion
  80.4 0.7 fusion.37
  81.0 0.1 fusion.40
  81.1 0.1 pad_maximum_fusion.10
  81.2 0.6 fusion.43
  81.8 0.1 fusion.39
  81.9 0.1 pad_maximum_fusion.6
  82.0 0.6 fusion.42
  82.6 0.2 pad_maximum_fusion.4
  82.8 0.6 fusion.41
  83.4 0.6 convolution_add_fusion.3
  84.0 0.1 pad_maximum_fusion.8
  84.1 0.6 convolution_add_fusion.5
  84.7 0.6 convolution_add_fusion.7
  85.3 0.1 pad_maximum_fusion.12
  85.4 0.6 fusion.18
  86.0 0.6 fusion.19
  86.7 0.6 fusion.20
  87.3 0.3 copy-done.5
  87.6 0.1 copy-done.8
  87.8 0.8 fusion.17
  88.6 0.1 reshape.139
  88.7 0.1 copy.19
  88.8 0.5 broadcast_in_dim.6
  89.3 1.3 slice.254
  90.6 1.9 %collective-permute-start.2 = (bf16[4,1,320,384]{3,2,0,1:T(8,128)(2,1)}, bf16[4,1,320,384]{3,2,0,1:T(8,128)(2,1)S(1)}, u32[]{:S(2)}, u32[]{:S(2)}) collective-permute-start(bf16[4,1,320,384]{3,2,0,1:T(8,128)(2,1)} %slice.254), channel_id=1, source_target_pairs={{0,1},{1,2},{2,3},{3,4},{4,5},{5,6},{6,7},{7,8},{8,9},{9,10},{10,1... | collective-permute-start | bytes 2949128 | tf_op jit(solution)/shard_map/ppermute | solution.py:25
  92.6 2.6 %collective-permute-start.3 = (bf16[4,1,320,384]{3,2,0,1:T(8,128)(2,1)}, bf16[4,1,320,384]{3,2,0,1:T(8,128)(2,1)S(1)}, u32[]{:S(2)}, u32[]{:S(2)}) collective-permute-start(bf16[4,1,320,384]{3,2,0,1:T(8,128)(2,1)} %slice.254), channel_id=1, source_target_pairs={{1,0},{2,1},{3,2},{4,3},{5,4},{6,5},{7,6},{8,7},{9,8},{10,9},{11,1... | collective-permute-start | bytes 2949128 | tf_op jit(solution)/shard_map/ppermute | solution.py:26
  95.2 1.4 %fusion.38 = (bf16[1,3,384,192]{2,3,1,0:T(8,128)(2,1)S(1)}, bf16[1,3,384,192]{2,3,1,0:T(8,128)(2,1)S(1)}, bf16[1,3,384,192]{2,3,1,0:T(8,128)(2,1)S(1)}) fusion(bf16[3,3,384,192]{2,3,1,0:T(8,128)(2,1)} %param.20), kind=kLoop, calls=%fused_computation.74 | loop fusion | bytes 2654208 | tf_op jit(solution)/shard_map/slice | solution.py:44
  96.6 0.4 copy.24
  97.0 0.9 copy.29
  97.9 0.4 copy.26
  98.3 0.9 copy.30
  99.1 0.4 copy.23
  99.5 0.9 copy.28
  100.4 1.3 broadcast_in_dim.14
  101.7 2.2 %collective-permute-done.2 = bf16[4,1,320,384]{3,2,0,1:T(8,128)(2,1)S(1)} collective-permute-done((bf16[4,1,320,384]{3,2,0,1:T(8,128)(2,1)}, bf16[4,1,320,384]{3,2,0,1:T(8,128)(2,1)S(1)}, u32[]{:S(2)}, u32[]{:S(2)}) %collective-permute-start.2) | collective-permute-done | bytes 983072 | tf_op jit(solution)/shard_map/ppermute | solution.py:25
  103.9 6.4 %collective-permute-done.3 = bf16[4,1,320,384]{3,2,0,1:T(8,128)(2,1)S(1)} collective-permute-done((bf16[4,1,320,384]{3,2,0,1:T(8,128)(2,1)}, bf16[4,1,320,384]{3,2,0,1:T(8,128)(2,1)S(1)}, u32[]{:S(2)}, u32[]{:S(2)}) %collective-permute-start.3) | collective-permute-done | bytes 983072 | tf_op jit(solution)/shard_map/ppermute | solution.py:26
  110.3 1.7 %broadcast_in_dim.15 = bf16[4,2,320,384]{3,2,1,0:T(8,128)(2,1)S(1)} broadcast(bf16[4,320,384]{2,1,0:T(8,128)(2,1)} %broadcast_in_dim.14), dimensions={0,2,3} | broadcast | bytes 2949120 | tf_op jit(solution)/shard_map/broadcast_in_dim | solution.py:109
  112.1 1.3 fusion.9
  113.4 3.5 %fusion.36 = (bf16[4,2,320,384]{3,2,1,0:T(8,128)(2,1)S(1)}, bf16[4,2,320,384]{3,2,1,0:T(8,128)(2,1)S(1)}, bf16[4,2,320,384]{3,2,1,0:T(8,128)(2,1)S(1)}, bf16[4,2...) fusion(bf16[4,4,322,384]{3,2,1,0:T(8,128)(2,1)S(1)} %fusion.9), kind=kLoop, calls=%fused_computation.72 | loop fusion | bytes 23592960 | tf_op jit(solution)/shard_map/slice | solution.py:37
  116.9 5.8 %fusion.4 = (bf16[4,2,320,1152]{3,2,1,0:T(8,128)(2,1)S(1)}, bf16[4,2,320,1152]{3,2,1,0:T(8,128)(2,1)S(1)}, bf16[4,2,320,1152]{3,2,1,0:T(8,128)(2,1)S(1)}) fusion(bf16[4,2,320,384]{3,2,1,0:T(8,128)(2,1)S(1)} %broadcast_in_dim.15, bf16[4,1,320,384]{3,2,1,0:T(8,128)(2,1)} %bitcast.81, bf16[4,2,320,384]{3,2,1,0:T(8,128)(2,1)} %get-tuple-element.26, ...), kind=kLoop, calls=%fused_computation.8 | loop fusion | flops 64880640 | bytes 33423360 | tf_op jit(solution)/shard_map/concatenate | solution.py:35
  122.7 3.2 %fusion.44 = f32[2560,192]{0,1:T(8,128)S(1)} fusion(bf16[2560,1152]{1,0:T(8,128)(2,1)S(1)} %bitcast.79, bf16[1152,192]{0,1:T(8,128)(2,1)} %bitcast.107), kind=kOutput, calls=%fused_computation.80 | convolution fusion | flops 1132462080 | bytes 8306688 | tf_op jit(solution)/shard_map/dot_general | solution.py:42
  125.9 2.1 %fusion.45 = f32[2560,192]{0,1:T(8,128)S(1)} fusion(bf16[2560,1152]{1,0:T(8,128)(2,1)S(1)} %bitcast.78, bf16[1152,192]{0,1:T(8,128)(2,1)S(1)} %bitcast.108), kind=kOutput, calls=%fused_computation.81 | convolution fusion | flops 1132462080 | bytes 8306688 | tf_op jit(solution)/shard_map/dot_general | solution.py:42
  128.1 2.1 %fusion.12 = bf16[2560,192]{0,1:T(8,128)(2,1)S(1)} fusion(f32[2560,192]{0,1:T(8,128)S(1)} %fusion.45, f32[2560,192]{0,1:T(8,128)S(1)} %fusion.44, bf16[2560,1152]{1,0:T(8,128)(2,1)S(1)} %bitcast.77, bf16[1152,192]{0,1:T(8,128)(2,1)S(1)} %bitcast.109, f32[192]{0:T(256)S(1)} %copy-done.9), kind=kOutput, calls=%fused_computation.20 | convolution fusion | flops 1134428160 | bytes 11256576 | tf_op jit(solution)/shard_map/dot_general | solution.py:42
  130.2 2.1 %reshape.144 = bf16[4,2,320,192]{2,1,0,3:T(2,128)(2,1)} reshape(bf16[2560,192]{0,1:T(8,128)(2,1)S(1)} %fusion.12) | data formatting | bytes 1966080 | tf_op jit(solution)/shard_map/reshape | solution.py:113
  132.3 2.4 %copy.27 = bf16[4,2,320,192]{2,3,1,0:T(8,128)(2,1)} copy(bf16[4,2,320,192]{2,1,0,3:T(2,128)(2,1)} %reshape.144) | data formatting | bytes 1966080 | tf_op jit(solution)/shard_map/reshape | solution.py:113
  (27 shorter events, 0.2 us)
Async XLA Ops:
  0.0 87.7 %copy-start = (bf16[3,384,768]{2,1,0:T(8,128)(2,1)S(1)}, bf16[3,384,768]{2,1,0:T(8,128)(2,1)}, u32[]{:S(2)}) copy-start(bf16[3,384,768]{2,1,0:T(8,128)(2,1)} %param.18) | copy-start | bytes 5308420
  0.0 69.6 %copy-start.4 = (bf16[2,1,160,384]{3,2,1,0:T(8,128)(2,1)S(1)}, bf16[2,1,160,384]{3,2,1,0:T(8,128)(2,1)}, u32[]{:S(2)}) copy-start(bf16[2,1,160,384]{3,2,1,0:T(8,128)(2,1)} %param.12) | copy-start | bytes 737284
  63.9 9.7 %collective-permute-start = (bf16[4,1,160,384]{3,2,1,0:T(8,128)(2,1)S(1)}, bf16[4,1,160,384]{3,2,1,0:T(8,128)(2,1)S(1)}, u32[]{:S(2)}, u32[]{:S(2)}) collective-permute-start(bf16[4,1,160,384]{3,2,1,0:T(8,128)(2,1)S(1)} %pad_maximum_fusion.13), channel_id=1, source_target_pairs={{0,1},{1,2},{2,3},{3,4},{4,5},{5,6},{6,7},{7,8},{8,9},{9,10},{10,1... | collective-permute-start | bytes 1474568 | tf_op jit(solution)/shard_map/ppermute | solution.py:25
  67.6 12.3 %collective-permute-start.1 = (bf16[4,1,160,384]{3,2,1,0:T(8,128)(2,1)S(1)}, bf16[4,1,160,384]{3,2,1,0:T(8,128)(2,1)S(1)}, u32[]{:S(2)}, u32[]{:S(2)}) collective-permute-start(bf16[4,1,160,384]{3,2,1,0:T(8,128)(2,1)S(1)} %pad_maximum_fusion.13), channel_id=1, source_target_pairs={{1,0},{2,1},{3,2},{4,3},{5,4},{6,5},{7,6},{8,7},{9,8},{10,9},{11,1... | collective-permute-start | bytes 1474568 | tf_op jit(solution)/shard_map/ppermute | solution.py:26
  84.7 0.7 copy-start.10
  86.6 0.9 copy-start.5
  86.6 1.1 copy-start.8
  86.6 1.1 copy-start.11
  90.6 13.3 %collective-permute-start.2 = (bf16[4,1,320,384]{3,2,0,1:T(8,128)(2,1)}, bf16[4,1,320,384]{3,2,0,1:T(8,128)(2,1)S(1)}, u32[]{:S(2)}, u32[]{:S(2)}) collective-permute-start(bf16[4,1,320,384]{3,2,0,1:T(8,128)(2,1)} %slice.254), channel_id=1, source_target_pairs={{0,1},{1,2},{2,3},{3,4},{4,5},{5,6},{6,7},{7,8},{8,9},{9,10},{10,1... | collective-permute-start | bytes 2949128 | tf_op jit(solution)/shard_map/ppermute | solution.py:25
  92.6 17.8 %collective-permute-start.3 = (bf16[4,1,320,384]{3,2,0,1:T(8,128)(2,1)}, bf16[4,1,320,384]{3,2,0,1:T(8,128)(2,1)S(1)}, u32[]{:S(2)}, u32[]{:S(2)}) collective-permute-start(bf16[4,1,320,384]{3,2,0,1:T(8,128)(2,1)} %slice.254), channel_id=1, source_target_pairs={{1,0},{2,1},{3,2},{4,3},{5,4},{6,5},{7,6},{8,7},{9,8},{10,9},{11,1... | collective-permute-start | bytes 2949128 | tf_op jit(solution)/shard_map/ppermute | solution.py:26
  103.9 8.2 %copy-start.2 = (bf16[4,1,320,384]{3,2,0,1:T(8,128)(2,1)}, bf16[4,1,320,384]{3,2,0,1:T(8,128)(2,1)S(1)}, u32[]{:S(2)}) copy-start(bf16[4,1,320,384]{3,2,0,1:T(8,128)(2,1)S(1)} %collective-permute-done.2) | copy-start | bytes 2949124
  110.3 1.7 %copy-start.3 = (bf16[4,1,320,384]{3,2,0,1:T(8,128)(2,1)}, bf16[4,1,320,384]{3,2,0,1:T(8,128)(2,1)S(1)}, u32[]{:S(2)}) copy-start(bf16[4,1,320,384]{3,2,0,1:T(8,128)(2,1)S(1)} %collective-permute-done.3) | copy-start | bytes 2949124
  122.7 3.2 %copy-start.6 = (bf16[24,8,3,384]{3,1,2,0:T(8,128)(2,1)S(1)}, bf16[24,8,3,384]{3,1,2,0:T(8,128)(2,1)}, u32[]{:S(2)}) copy-start(bf16[24,8,3,384]{3,1,2,0:T(8,128)(2,1)} %copy.30) | copy-start | bytes 1327108
  125.9 2.1 %copy-start.7 = (bf16[24,8,3,384]{3,1,2,0:T(8,128)(2,1)S(1)}, bf16[24,8,3,384]{3,1,2,0:T(8,128)(2,1)}, u32[]{:S(2)}) copy-start(bf16[24,8,3,384]{3,1,2,0:T(8,128)(2,1)} %copy.28) | copy-start | bytes 1327108
  125.9 2.1 %copy-start.9 = (f32[192]{0:T(256)S(1)}, f32[192]{0:T(256)}, u32[]{:S(2)}) copy-start(f32[192]{0:T(256)} %param.21) | copy-start | bytes 2308
  128.1 6.6 %copy-start.1 = (bf16[3,384,768]{2,1,0:T(8,128)(2,1)S(1)}, bf16[3,384,768]{2,1,0:T(8,128)(2,1)}, u32[]{:S(2)}) copy-start(bf16[3,384,768]{2,1,0:T(8,128)(2,1)} %param.18) | copy-start | bytes 5308420
where the time goes:
time: 135 us
  blocking collectives  59.7 us (44%)
  local copies, waits for them, and re-layouts  24 us (18%)
  waiting for transfers between devices  14.9 us (11%)
  matrix products  13.5 us (10%)
  other arithmetic  11.9 us (9%)
  starting transfers between devices  10.3 us (8%)
    psum x3, blocking collectives, over_axes(): value = lax.psum(value, axis)  59.7 us
    ppermute x2, waiting for transfers between devices, with_halo(): after = lax.ppermute(initial, axis, down)  12.7 us
    dot_general x12, matrix products, conv_taps(): jnp.dot(window.reshape(-1, 3 * channels), kernel[row_tap].reshape(3 * cha...  12.7 us
    slice x5, local copies, waits for them, and re-layouts, conv_taps(): kernel[row_tap].reshape(3 * channels, -1)  6.51 us
    concatenate x6, other arithmetic, conv_taps(): jnp.concatenate([padded[:, row_tap:row_tap + row_count, col_tap:col_tap +...  6.42 us
    ppermute x2, starting transfers between devices, with_halo(): before = lax.ppermute(last, axis, up)  5.69 us
    ppermute x2, starting transfers between devices, with_halo(): after = lax.ppermute(initial, axis, down)  4.57 us
    reshape x2, local copies, waits for them, and re-layouts, on_device(): result.astype(jnp.bfloat16)  4.54 us
  transfers between devices with their start and end apart: 4, of which 3 were waited for; matrix products, arithmetic and copies ran while one was open for 8% of the time, Pallas kernels for 0%

commit v1 on v0

--- a/solution.py
+++ b/solution.py
@@ -11,7 +11,7 @@
 
 def over_axes(value, axes):
     for axis in axes:
-        value = lax.psum(value, axis)
+        value = jnp.sum(lax.all_gather(value, axis), axis=0)
     return value
 
 

time: 135 us -> 143 us (1.059)
  local copies, waits for them, and re-layouts: 24 us -> 29.5 us
  between operations: 0.44 us -> 2.42 us
    psum x3 -> x0, blocking collectives: 59.7 us -> none  [over_axes(): value = lax.psum(value, axis)]
    unnamed x0 -> x3, blocking collectives: none -> 59.6 us
    unnamed x27 -> x42, local copies, waits for them, and re-layouts: 3.04 us -> 8.12 us
  transfers between devices with their start and end apart: 4 -> 4, of which waited for: 3 -> 3; matrix products, arithmetic and copies ran while one was open for 8% -> 7% of each run, Pallas kernels for 0% -> 0%
where the time goes in v1:
time: 143 us; the launch traced here: 142 us
  blocking collectives  59.6 us (42%)
  local copies, waits for them, and re-layouts  29.5 us (21%)
  waiting for transfers between devices  15 us (10%)
  matrix products  13.5 us (9%)
  other arithmetic  12 us (8%)
  starting transfers between devices  10.2 us (7%)
  between operations  2.42 us (2%)
    unnamed x3, blocking collectives  59.6 us
    ppermute x2, waiting for transfers between devices, with_halo(): after = lax.ppermute(initial, axis, down)  12.7 us
    dot_general x12, matrix products, conv_taps(): jnp.dot(window.reshape(-1, 3 * channels), kernel[row_tap].reshape(3 * cha...  12.7 us
    unnamed x42, local copies, waits for them, and re-layouts  8.12 us
    slice x5, local copies, waits for them, and re-layouts, conv_taps(): kernel[row_tap].reshape(3 * channels, -1)  6.51 us
    concatenate x6, other arithmetic, conv_taps(): jnp.concatenate([padded[:, row_tap:row_tap + row_count, col_tap:col_tap +...  6.42 us
    ppermute x2, starting transfers between devices, with_halo(): before = lax.ppermute(last, axis, up)  5.68 us
    ppermute x2, starting transfers between devices, with_halo(): after = lax.ppermute(initial, axis, down)  4.57 us
  transfers between devices with their start and end apart: 4, of which 3 were waited for; matrix products, arithmetic and copies ran while one was open for 7% of the time, Pallas kernels for 0%

profile of v1, /device:TPU:39, one launch (start us, length us, event | category | flops | bytes accessed | tf_op | source)
XLA Modules:
  0.0 142.4 jit_solution(709173864324018622)
XLA Ops:
  0.0 1.2 convert_reduce_fusion
  1.4 1.3 dynamic-slice
  3.3 0.1 reduce_sum.88
  3.4 0.1 reduce_sum.94
  3.6 0.2 dynamic-update-slice
  3.8 0.2 dynamic-update-slice.3
  4.0 42.4 %all-reduce.8 = (f32[512]{0:T(512)S(1)}, f32[512]{0:T(512)S(1)}) all-reduce(f32[512]{0:T(512)S(1)} %dynamic-update-slice.3, f32[512]{0:T(512)S(1)} %dynamic-update-slice), channel_id=5, replica_groups=mesh['parts'=2,'rows_0'=16,'rows_1'=4,'rows_2'=2] {'rows_0'}, use_global_device_ids=true, to_apply=%add.5 | all-reduce | flops 1024 | bytes 8192
  46.5 1.3 dynamic-slice.1
  48.5 0.2 dynamic-update-slice.1
  48.7 0.2 dynamic-update-slice.4
  48.9 5.8 %all-reduce.9 = (f32[128]{0:T(128)S(1)}, f32[128]{0:T(128)S(1)}) all-reduce(f32[128]{0:T(128)S(1)} %dynamic-update-slice.4, f32[128]{0:T(128)S(1)} %dynamic-update-slice.1), channel_id=6, replica_groups=mesh['parts'=2,'rows_0'=16,'rows_1'=4,'rows_2'=2] {'rows_1'}, use_global_device_ids=true, to_apply=%add.6 | all-reduce | flops 256 | bytes 2048
  54.8 1.3 dynamic-slice.2
  56.8 0.2 dynamic-update-slice.2
  57.1 0.2 dynamic-update-slice.5
  57.3 11.5 %all-reduce.10 = (f32[64]{0:T(128)S(1)}, f32[64]{0:T(128)S(1)}) all-reduce(f32[64]{0:T(128)S(1)} %dynamic-update-slice.5, f32[64]{0:T(128)S(1)} %dynamic-update-slice.2), channel_id=7, replica_groups=mesh['parts'=2,'rows_0'=16,'rows_1'=4,'rows_2'=2] {'rows_2'}, use_global_device_ids=true, to_apply=%add.7 | all-reduce | flops 128 | bytes 1024
  69.1 0.1 mul.49
  69.3 0.1 sub.25
  69.4 1.1 fusion.31
  70.5 1.0 pad_maximum_fusion.13
  71.5 3.7 %collective-permute-start = (bf16[4,1,160,384]{3,2,1,0:T(8,128)(2,1)S(1)}, bf16[4,1,160,384]{3,2,1,0:T(8,128)(2,1)S(1)}, u32[]{:S(2)}, u32[]{:S(2)}) collective-permute-start(bf16[4,1,160,384]{3,2,1,0:T(8,128)(2,1)S(1)} %pad_maximum_fusion.13), channel_id=1, source_target_pairs={{0,1},{1,2},{2,3},{3,4},{4,5},{5,6},{6,7},{7,8},{8,9},{9,10},{10,1... | collective-permute-start | bytes 1474568 | tf_op jit(solution)/shard_map/ppermute | solution.py:25
  75.3 2.0 %collective-permute-start.1 = (bf16[4,1,160,384]{3,2,1,0:T(8,128)(2,1)S(1)}, bf16[4,1,160,384]{3,2,1,0:T(8,128)(2,1)S(1)}, u32[]{:S(2)}, u32[]{:S(2)}) collective-permute-start(bf16[4,1,160,384]{3,2,1,0:T(8,128)(2,1)S(1)} %pad_maximum_fusion.13), channel_id=1, source_target_pairs={{1,0},{2,1},{3,2},{4,3},{5,4},{6,5},{7,6},{8,7},{9,8},{10,9},{11,1... | collective-permute-start | bytes 1474568 | tf_op jit(solution)/shard_map/ppermute | solution.py:26
  77.3 3.9 %fusion.35 = (bf16[1,1,3,384,384]{4,3,2,1,0:T(8,128)(2,1)S(1)}, bf16[1,1,3,384,384]{4,3,2,1,0:T(8,128)(2,1)S(1)}, bf16[1,1,3,384,384]{4,3,2,1,0:T(8,128)(2,1)S(1...) fusion(bf16[3,3,3,384,384]{4,3,2,1,0:T(8,128)(2,1)} %param.16), kind=kLoop, calls=%fused_computation.71 | loop fusion | bytes 15925248 | tf_op jit(solution)/shard_map/slice | solution.py:44
  81.3 6.3 %collective-permute-done.1 = bf16[4,1,160,384]{3,2,1,0:T(8,128)(2,1)S(1)} collective-permute-done((bf16[4,1,160,384]{3,2,1,0:T(8,128)(2,1)S(1)}, bf16[4,1,160,384]{3,2,1,0:T(8,128)(2,1)S(1)}, u32[]{:S(2)}, u32[]{:S(2)}) %collective-permute-start.1) | collective-permute-done | bytes 491552 | tf_op jit(solution)/shard_map/ppermute | solution.py:26
  87.6 0.5 select_maximum_fusion
  88.0 0.7 fusion.37
  88.8 0.1 pad_maximum_fusion.10
  88.9 0.6 fusion.43
  89.6 0.1 pad_maximum_fusion.6
  89.7 0.6 fusion.42
  90.3 0.2 pad_maximum_fusion.4
  90.5 0.6 fusion.41
  91.1 0.6 convolution_add_fusion.3
  91.6 0.1 pad_maximum_fusion.8
  91.8 0.6 convolution_add_fusion.5
  92.4 0.6 convolution_add_fusion.7
  93.1 0.6 fusion.18
  93.7 0.6 fusion.19
  94.3 0.6 fusion.20
  94.9 0.3 copy-done.5
  95.4 0.8 fusion.17
  96.3 0.1 reshape.149
  96.4 0.5 broadcast_in_dim.6
  97.0 1.3 slice.254
  98.3 1.9 %collective-permute-start.2 = (bf16[4,1,320,384]{3,2,0,1:T(8,128)(2,1)}, bf16[4,1,320,384]{3,2,0,1:T(8,128)(2,1)S(1)}, u32[]{:S(2)}, u32[]{:S(2)}) collective-permute-start(bf16[4,1,320,384]{3,2,0,1:T(8,128)(2,1)} %slice.254), channel_id=1, source_target_pairs={{0,1},{1,2},{2,3},{3,4},{4,5},{5,6},{6,7},{7,8},{8,9},{9,10},{10,1... | collective-permute-start | bytes 2949128 | tf_op jit(solution)/shard_map/ppermute | solution.py:25
  100.2 2.6 %collective-permute-start.3 = (bf16[4,1,320,384]{3,2,0,1:T(8,128)(2,1)}, bf16[4,1,320,384]{3,2,0,1:T(8,128)(2,1)S(1)}, u32[]{:S(2)}, u32[]{:S(2)}) collective-permute-start(bf16[4,1,320,384]{3,2,0,1:T(8,128)(2,1)} %slice.254), channel_id=1, source_target_pairs={{1,0},{2,1},{3,2},{4,3},{5,4},{6,5},{7,6},{8,7},{9,8},{10,9},{11,1... | collective-permute-start | bytes 2949128 | tf_op jit(solution)/shard_map/ppermute | solution.py:26
  102.8 1.4 fusion.38
  104.3 0.4 copy.34
  104.7 0.9 copy.39
  105.5 0.4 copy.36
  105.9 0.8 copy.40
  106.7 0.4 copy.33
  107.1 0.9 copy.38
  108.0 1.3 broadcast_in_dim.14
  109.3 2.3 %collective-permute-done.2 = bf16[4,1,320,384]{3,2,0,1:T(8,128)(2,1)S(1)} collective-permute-done((bf16[4,1,320,384]{3,2,0,1:T(8,128)(2,1)}, bf16[4,1,320,384]{3,2,0,1:T(8,128)(2,1)S(1)}, u32[]{:S(2)}, u32[]{:S(2)}) %collective-permute-start.2) | collective-permute-done | bytes 983072 | tf_op jit(solution)/shard_map/ppermute | solution.py:25
  111.6 6.4 %collective-permute-done.3 = bf16[4,1,320,384]{3,2,0,1:T(8,128)(2,1)S(1)} collective-permute-done((bf16[4,1,320,384]{3,2,0,1:T(8,128)(2,1)}, bf16[4,1,320,384]{3,2,0,1:T(8,128)(2,1)S(1)}, u32[]{:S(2)}, u32[]{:S(2)}) %collective-permute-start.3) | collective-permute-done | bytes 983072 | tf_op jit(solution)/shard_map/ppermute | solution.py:26
  118.0 1.7 %broadcast_in_dim.15 = bf16[4,2,320,384]{3,2,1,0:T(8,128)(2,1)S(1)} broadcast(bf16[4,320,384]{2,1,0:T(8,128)(2,1)} %broadcast_in_dim.14), dimensions={0,2,3} | broadcast | bytes 2949120 | tf_op jit(solution)/shard_map/broadcast_in_dim | solution.py:109
  119.7 1.3 fusion.9
  121.1 3.5 %fusion.36 = (bf16[4,2,320,384]{3,2,1,0:T(8,128)(2,1)S(1)}, bf16[4,2,320,384]{3,2,1,0:T(8,128)(2,1)S(1)}, bf16[4,2,320,384]{3,2,1,0:T(8,128)(2,1)S(1)}, bf16[4,2...) fusion(bf16[4,4,322,384]{3,2,1,0:T(8,128)(2,1)S(1)} %fusion.9), kind=kLoop, calls=%fused_computation.72 | loop fusion | bytes 23592960 | tf_op jit(solution)/shard_map/slice | solution.py:37
  124.5 5.8 %fusion.4 = (bf16[4,2,320,1152]{3,2,1,0:T(8,128)(2,1)S(1)}, bf16[4,2,320,1152]{3,2,1,0:T(8,128)(2,1)S(1)}, bf16[4,2,320,1152]{3,2,1,0:T(8,128)(2,1)S(1)}) fusion(bf16[4,2,320,384]{3,2,1,0:T(8,128)(2,1)S(1)} %broadcast_in_dim.15, bf16[4,1,320,384]{3,2,1,0:T(8,128)(2,1)} %bitcast.84, bf16[4,2,320,384]{3,2,1,0:T(8,128)(2,1)} %get-tuple-element.26, ...), kind=kLoop, calls=%fused_computation.8 | loop fusion | flops 64880640 | bytes 33423360 | tf_op jit(solution)/shard_map/concatenate | solution.py:35
  130.4 3.2 %fusion.44 = f32[2560,192]{0,1:T(8,128)S(1)} fusion(bf16[2560,1152]{1,0:T(8,128)(2,1)S(1)} %bitcast.82, bf16[1152,192]{0,1:T(8,128)(2,1)} %bitcast.110), kind=kOutput, calls=%fused_computation.80 | convolution fusion | flops 1132462080 | bytes 8306688 | tf_op jit(solution)/shard_map/dot_general | solution.py:42
  133.6 2.1 %fusion.45 = f32[2560,192]{0,1:T(8,128)S(1)} fusion(bf16[2560,1152]{1,0:T(8,128)(2,1)S(1)} %bitcast.81, bf16[1152,192]{0,1:T(8,128)(2,1)S(1)} %bitcast.111), kind=kOutput, calls=%fused_computation.81 | convolution fusion | flops 1132462080 | bytes 8306688 | tf_op jit(solution)/shard_map/dot_general | solution.py:42
  135.7 2.1 %fusion.12 = bf16[2560,192]{0,1:T(8,128)(2,1)S(1)} fusion(f32[2560,192]{0,1:T(8,128)S(1)} %fusion.45, f32[2560,192]{0,1:T(8,128)S(1)} %fusion.44, bf16[2560,1152]{1,0:T(8,128)(2,1)S(1)} %bitcast.80, bf16[1152,192]{0,1:T(8,128)(2,1)S(1)} %bitcast.112, f32[192]{0:T(256)S(1)} %copy-done.9), kind=kOutput, calls=%fused_computation.20 | convolution fusion | flops 1134428160 | bytes 11256576 | tf_op jit(solution)/shard_map/dot_general | solution.py:42
  137.8 2.1 %reshape.154 = bf16[4,2,320,192]{2,1,0,3:T(2,128)(2,1)} reshape(bf16[2560,192]{0,1:T(8,128)(2,1)S(1)} %fusion.12) | data formatting | bytes 1966080 | tf_op jit(solution)/shard_map/reshape | solution.py:113
  139.9 2.4 %copy.37 = bf16[4,2,320,192]{2,3,1,0:T(8,128)(2,1)} copy(bf16[4,2,320,192]{2,1,0,3:T(2,128)(2,1)} %reshape.154) | data formatting | bytes 1966080 | tf_op jit(solution)/shard_map/reshape | solution.py:113
  (54 shorter events, 1.5 us)
Async XLA Ops:
  0.0 95.4 %copy-start = (bf16[3,384,768]{2,1,0:T(8,128)(2,1)S(1)}, bf16[3,384,768]{2,1,0:T(8,128)(2,1)}, u32[]{:S(2)}) copy-start(bf16[3,384,768]{2,1,0:T(8,128)(2,1)} %param.18) | copy-start | bytes 5308420
  0.0 77.2 %copy-start.4 = (bf16[2,1,160,384]{3,2,1,0:T(8,128)(2,1)S(1)}, bf16[2,1,160,384]{3,2,1,0:T(8,128)(2,1)}, u32[]{:S(2)}) copy-start(bf16[2,1,160,384]{3,2,1,0:T(8,128)(2,1)} %param.12) | copy-start | bytes 737284
  71.5 9.7 %collective-permute-start = (bf16[4,1,160,384]{3,2,1,0:T(8,128)(2,1)S(1)}, bf16[4,1,160,384]{3,2,1,0:T(8,128)(2,1)S(1)}, u32[]{:S(2)}, u32[]{:S(2)}) collective-permute-start(bf16[4,1,160,384]{3,2,1,0:T(8,128)(2,1)S(1)} %pad_maximum_fusion.13), channel_id=1, source_target_pairs={{0,1},{1,2},{2,3},{3,4},{4,5},{5,6},{6,7},{7,8},{8,9},{9,10},{10,1... | collective-permute-start | bytes 1474568 | tf_op jit(solution)/shard_map/ppermute | solution.py:25
  75.3 12.3 %collective-permute-start.1 = (bf16[4,1,160,384]{3,2,1,0:T(8,128)(2,1)S(1)}, bf16[4,1,160,384]{3,2,1,0:T(8,128)(2,1)S(1)}, u32[]{:S(2)}, u32[]{:S(2)}) collective-permute-start(bf16[4,1,160,384]{3,2,1,0:T(8,128)(2,1)S(1)} %pad_maximum_fusion.13), channel_id=1, source_target_pairs={{1,0},{2,1},{3,2},{4,3},{5,4},{6,5},{7,6},{8,7},{9,8},{10,9},{11,1... | collective-permute-start | bytes 1474568 | tf_op jit(solution)/shard_map/ppermute | solution.py:26
  92.4 0.7 copy-start.10
  94.3 0.9 copy-start.5
  94.3 1.1 copy-start.8
  94.3 1.1 copy-start.11
  98.3 13.3 %collective-permute-start.2 = (bf16[4,1,320,384]{3,2,0,1:T(8,128)(2,1)}, bf16[4,1,320,384]{3,2,0,1:T(8,128)(2,1)S(1)}, u32[]{:S(2)}, u32[]{:S(2)}) collective-permute-start(bf16[4,1,320,384]{3,2,0,1:T(8,128)(2,1)} %slice.254), channel_id=1, source_target_pairs={{0,1},{1,2},{2,3},{3,4},{4,5},{5,6},{6,7},{7,8},{8,9},{9,10},{10,1... | collective-permute-start | bytes 2949128 | tf_op jit(solution)/shard_map/ppermute | solution.py:25
  100.2 17.8 %collective-permute-start.3 = (bf16[4,1,320,384]{3,2,0,1:T(8,128)(2,1)}, bf16[4,1,320,384]{3,2,0,1:T(8,128)(2,1)S(1)}, u32[]{:S(2)}, u32[]{:S(2)}) collective-permute-start(bf16[4,1,320,384]{3,2,0,1:T(8,128)(2,1)} %slice.254), channel_id=1, source_target_pairs={{1,0},{2,1},{3,2},{4,3},{5,4},{6,5},{7,6},{8,7},{9,8},{10,9},{11,1... | collective-permute-start | bytes 2949128 | tf_op jit(solution)/shard_map/ppermute | solution.py:26
  111.6 8.2 %copy-start.2 = (bf16[4,1,320,384]{3,2,0,1:T(8,128)(2,1)}, bf16[4,1,320,384]{3,2,0,1:T(8,128)(2,1)S(1)}, u32[]{:S(2)}) copy-start(bf16[4,1,320,384]{3,2,0,1:T(8,128)(2,1)S(1)} %collective-permute-done.2) | copy-start | bytes 2949124
  118.0 1.7 %copy-start.3 = (bf16[4,1,320,384]{3,2,0,1:T(8,128)(2,1)}, bf16[4,1,320,384]{3,2,0,1:T(8,128)(2,1)S(1)}, u32[]{:S(2)}) copy-start(bf16[4,1,320,384]{3,2,0,1:T(8,128)(2,1)S(1)} %collective-permute-done.3) | copy-start | bytes 2949124
  130.4 3.2 %copy-start.6 = (bf16[24,8,3,384]{3,1,2,0:T(8,128)(2,1)S(1)}, bf16[24,8,3,384]{3,1,2,0:T(8,128)(2,1)}, u32[]{:S(2)}) copy-start(bf16[24,8,3,384]{3,1,2,0:T(8,128)(2,1)} %copy.40) | copy-start | bytes 1327108
  133.6 2.1 %copy-start.7 = (bf16[24,8,3,384]{3,1,2,0:T(8,128)(2,1)S(1)}, bf16[24,8,3,384]{3,1,2,0:T(8,128)(2,1)}, u32[]{:S(2)}) copy-start(bf16[24,8,3,384]{3,1,2,0:T(8,128)(2,1)} %copy.38) | copy-start | bytes 1327108
  133.6 2.1 %copy-start.9 = (f32[192]{0:T(256)S(1)}, f32[192]{0:T(256)}, u32[]{:S(2)}) copy-start(f32[192]{0:T(256)} %param.21) | copy-start | bytes 2308
  135.7 6.6 %copy-start.1 = (bf16[3,384,768]{2,1,0:T(8,128)(2,1)S(1)}, bf16[3,384,768]{2,1,0:T(8,128)(2,1)}, u32[]{:S(2)}) copy-start(bf16[3,384,768]{2,1,0:T(8,128)(2,1)} %param.18) | copy-start | bytes 5308420
